TPU v7x, 32 devices: a whole 2x2x4 slice. The times are simulated.
32 devices in a mesh: psr: 8 (over z, x), toa: 4 (over y, core).
Axes of the slice: x: 2, y: 2, z: 4, core: 2. Of those that a mesh axis runs over, the one named last changes fastest.
Arguments:
- design: bfloat16 [3072, 128, 256], P(('psr', 'toa')), may hold values from -0.035888672 to 0.035888672
- noise_weight: float32 [3072, 128], P(('psr', 'toa')), may hold values from 0.3 to 3
- residuals: bfloat16 [3072, 128], P(('psr', 'toa')), may hold values from -6 to 6
- slot_pulsar: int32 [3072], P(('psr', 'toa')), may hold values from 0 to 7, as said below
- slot_rows: int32 [3072], P(('psr', 'toa')), may hold values from 0 to 128, as said below
- own_prior: float32 [64, 192], P(('psr', 'toa')), may hold values from 0.2 to 5
- spectrum: float32 [32], replicated, may hold values from 0.05 to 2
- directions: float32 [3, 64], replicated, may hold values from -1 to 1, as said below
Outputs:
- coeffs: float32 [64, 64], P(('psr', 'toa'))
- log_dets: float32 [64], P(('psr', 'toa'))
- chi_square: float32 [64], P(('psr', 'toa'))
Inputs may be any that keep to these rules, and one draw needn't show every extreme that they name: `slot_pulsar`: pulsar k of group g is pulsar g * 8 + k of the arrays with a pulsar dimension; empty blocks name pulsar 0. `slot_rows`: on each device the blocks holding TOAs come first and the empty ones (0 rows) last; within a psr group a pulsar's blocks are consecutive in device order, cyclically, all full but its last; every pulsar has between 4 * 96 * 4 and 4 * 96 * 16 TOAs. `directions`: unit vectors; any two are at least 0.1 radians apart.
All inputs are finite; a program needn't handle non-finite values.
Results may differ from a plain program's by a relative error of at most 0.003.
Values sent between devices are 32-bit elements; how exact they have to be, the bound alone decides.
A program may use at most 128 MiB of HBM per device.

v0:
```python
import jax
import jax.numpy as jnp
from jax import lax
from jax.sharding import PartitionSpec as P

GROUP_PULSARS = 8
ITERS = 8


highest = lax.Precision.HIGHEST


def cholesky_solve(factor, right_side):
    halfway = lax.linalg.triangular_solve(factor, right_side, left_side=True, lower=True)
    return lax.linalg.triangular_solve(
        factor, halfway, left_side=True, lower=True, transpose_a=True
    )


def slot_term_values(design, weight, residuals, pulsar, slot_rows):
    positions = lax.broadcasted_iota(jnp.int32, weight.shape, 1)
    weight = jnp.where(positions < slot_rows[:, None], weight, 0.0)
    weighted = (weight[:, :, None] * design).astype(jnp.bfloat16)
    products = jnp.einsum("srk,srl->skl", weighted, design, preferred_element_type=jnp.float32)
    fitted = jnp.einsum("srk,sr->sk", weighted, residuals, preferred_element_type=jnp.float32)
    widened = residuals.astype(jnp.float32)
    energy = jnp.sum(weight * widened * widened, axis=1)
    owners = (
        pulsar[:, None] == lax.broadcasted_iota(jnp.int32, (pulsar.shape[0], GROUP_PULSARS), 1)
    ).astype(jnp.float32)
    return (
        jnp.einsum("sp,skl->pkl", owners, products, precision=highest),
        jnp.einsum("sp,sk->pk", owners, fitted, precision=highest),
        jnp.dot(energy, owners, precision=highest),
        jnp.dot(slot_rows.astype(jnp.float32), owners, precision=highest),
    )


def local_grams(design, noise_weight, residuals, slot_pulsar, slot_rows):
    column_count = design.shape[2]
    used_slots = jnp.sum((slot_rows > 0).astype(jnp.int32))
    block_count = (used_slots + 15) // 16
    initial = (
        jnp.zeros((GROUP_PULSARS, column_count, column_count), jnp.float32),
        jnp.zeros((GROUP_PULSARS, column_count), jnp.float32),
        jnp.zeros((GROUP_PULSARS,), jnp.float32),
        jnp.zeros((GROUP_PULSARS,), jnp.float32),
    )

    def one_block(block_index, running_total):
        offset = block_index * 16
        term_pieces = [
            lax.dynamic_slice_in_dim(member, offset, 16, 0)
            for member in (design, noise_weight, residuals, slot_pulsar, slot_rows)
        ]
        summand_terms = slot_term_values(*term_pieces)
        return tuple(
            (
                earlier_term + later_term
                for earlier_term, later_term in zip(running_total, summand_terms)
            )
        )

    return lax.fori_loop(0, block_count, one_block, initial)


def eliminate(gram_sums, projections, own_prior):
    column_count = gram_sums.shape[1]
    common = column_count - own_prior.shape[1]
    identity = jnp.eye(own_prior.shape[1], dtype=jnp.float32)
    own_block = (
        gram_sums[:, common:, common:] + (1.0 / own_prior)[:, :, None] * identity[None, :, :]
    )
    factor = jnp.linalg.cholesky(own_block)
    right_side = jnp.concatenate(
        [gram_sums[:, common:, :common], projections[:, common:, None]], axis=2
    )
    solved = cholesky_solve(factor, right_side)
    cross_block = gram_sums[:, :common, common:]
    reduced = jnp.einsum("pck,pkd->pcd", cross_block, solved, precision=highest)
    schur_part = gram_sums[:, :common, :common] - reduced[:, :, :common]
    target = projections[:, :common] - reduced[:, :, common]
    quadratic = jnp.sum(projections[:, common:] * solved[:, :, common], axis=1)
    own_logdet = 2.0 * jnp.sum(jnp.log(jnp.diagonal(factor, axis1=1, axis2=2)), axis=1)
    return (schur_part, target, quadratic, own_logdet)


def coupling_inverse(directions):
    cosines = jnp.clip(jnp.dot(directions.T, directions, precision=highest), -1.0, 1.0)
    number = cosines.shape[0]
    diagonal = jnp.eye(number, dtype=jnp.float32) > 0.5
    spread = jnp.where(diagonal, 1.0, 0.5 * (1.0 - cosines))
    intersect_curve = 1.5 * spread * jnp.log(spread) - 0.25 * spread + 0.5
    correlation = jnp.where(diagonal, 1.0, intersect_curve)
    factor = jnp.linalg.cholesky(correlation)
    return cholesky_solve(factor, jnp.eye(number, dtype=jnp.float32))


def coupled_apply(schur_part, coupling, inverse_power, vector):
    within = jnp.einsum("pcd,pd->pc", schur_part, vector, precision=highest)
    mixing = jnp.dot(coupling, vector, precision=highest)
    return within + mixing * inverse_power[None, :]


def precondition(block_factor, residual):
    return cholesky_solve(block_factor, residual[:, :, None])[:, :, 0]


def block_setup(schur_part, self_coupling, inverse_power):
    block_matrix = schur_part + self_coupling[:, None, None] * jnp.diag(inverse_power)[None, :, :]
    block_factor = jnp.linalg.cholesky(block_matrix)
    block_logdet = 2.0 * jnp.sum(jnp.log(jnp.diagonal(block_factor, axis1=1, axis2=2)), axis=1)
    return (block_factor, block_logdet)


def conjugate(
    schur_part, target, self_coupling, inverse_power, apply_matrix, curvature_total, scaled_total
):
    block_factor, block_logdet = block_setup(schur_part, self_coupling, inverse_power)
    solution = jnp.zeros_like(target)
    residual = target
    scaled = precondition(block_factor, residual)
    direction = scaled
    inner_now = scaled_total(jnp.sum(residual * scaled))
    for iteration in range(ITERS):
        mapped = apply_matrix(direction)
        step_size = inner_now / curvature_total(jnp.sum(direction * mapped))
        solution = solution + step_size * direction
        residual = residual - step_size * mapped
        if iteration + 1 < ITERS:
            scaled = precondition(block_factor, residual)
            inner_next = scaled_total(jnp.sum(residual * scaled))
            direction = scaled + inner_next / inner_now * direction
            inner_now = inner_next
    return (solution, block_logdet)


def body(design, noise_weight, residuals, slot_pulsar, slot_rows, own_prior, spectrum, directions):
    toa_devices = lax.axis_size("toa")
    owned_count = GROUP_PULSARS // toa_devices
    device = lax.axis_index("psr") * toa_devices + lax.axis_index("toa")
    first_pulsar = device * owned_count
    gram_part, fit_part, energy_part, count_part = local_grams(
        design, noise_weight, residuals, slot_pulsar, slot_rows
    )
    reduced_ready = False
    totals = lax.psum((gram_part, fit_part, energy_part, count_part), "toa")
    first_local = lax.axis_index("toa") * owned_count
    gram_sums, projections, energy, counts = [
        lax.dynamic_slice_in_dim(member, first_local, owned_count, 0) for member in totals
    ]
    schur_part, target, quadratic, own_logdet = eliminate(gram_sums, projections, own_prior)
    coupling = coupling_inverse(directions)
    inverse_power = 1.0 / jnp.repeat(spectrum, 2)
    all_schur, all_target = (
        lax.all_gather(schur_part, ("psr", "toa"), axis=0, tiled=True),
        lax.all_gather(target, ("psr", "toa"), axis=0, tiled=True),
    )

    def apply_all(vector):
        return coupled_apply(all_schur, coupling, inverse_power, vector)

    def plain_total(value):
        return value

    whole_solution, whole_logdet = conjugate(
        all_schur,
        all_target,
        jnp.diagonal(coupling),
        inverse_power,
        apply_all,
        plain_total,
        plain_total,
    )
    solution = lax.dynamic_slice_in_dim(whole_solution, first_pulsar, owned_count, 0)
    block_logdet = lax.dynamic_slice_in_dim(whole_logdet, first_pulsar, owned_count, 0)
    column_count = design.shape[2]
    log_dets = (own_logdet + block_logdet) / column_count
    chi_square = (energy - quadratic - jnp.sum(target * solution, axis=1)) / counts
    return (solution, log_dets, chi_square)


def solution(mesh):
    return jax.shard_map(
        body,
        mesh=mesh,
        in_specs=(
            P(("psr", "toa"), None, None),
            P(("psr", "toa"), None),
            P(("psr", "toa"), None),
            P(("psr", "toa")),
            P(("psr", "toa")),
            P(("psr", "toa"), None),
            P(),
            P(),
        ),
        out_specs=(P(("psr", "toa"), None), P(("psr", "toa")), P(("psr", "toa"))),
        check_vma=False,
    )
```

profile of v0, /device:TPU:0, one launch (start us, length us, event | category | flops | bytes accessed | tf_op | source)
XLA Modules:
  0.0 903.3 jit_solution(16755059982066473360)
XLA Ops:
  9.4 67.4 %while.18 = (s32[]{:T(128)}, f32[8,256,256]{2,0,1:T(8,128)S(1)}, f32[8,256]{1,0:T(8,128)S(1)}, f32[8]{0:T(128)S(1)}, f32[8]{0:T(128)S(1)}, /*index=5*/s32[]{:T(1...) while((s32[]{:T(128)}, f32[8,256,256]{2,0,1:T(8,128)S(1)}, ...), condition=%wide.region_3.4_spmd, body=%wide.region_1.3_spmd.sunk | while | flops 374228512 | bytes 15829071 | solution.py:64
  13.1 4.8 fusion.191
  24.3 4.8 fusion.191
  69.3 4.8 fusion.191
  79.1 7.2 all-reduce.3
  86.4 5.8 cholesky.225
  92.4 40.5 %all-reduce.6.cloned.1.call-done = f32[8,256,256]{1,2,0:T(8,128)} async-done(((f32[8,256,256]{1,2,0:T(8,128)}), f32[8,256,256]{1,2,0:T(8,128)}) %all-reduce.6.cloned.1.call-update) | async-done | bytes 2097168 | tf_op jit(solution)/shard_map/psum | solution.py:147
  135.5 23.5 %custom-call.36 = f32[2,128,128]{2,1,0:T(8,128)S(1)} custom-call(f32[2,128,128]{2,1,0:T(8,128)S(1)} %cholesky.242), custom_call_target="Cholesky" | custom-call | tf_op jit(solution)/shard_map/jit(cholesky)/cholesky | solution.py:74
  159.0 19.7 %custom-call.37 = f32[2,1,128,128]{2,3,1,0:T(8,128)S(1)} custom-call(f32[2,1,128,128]{3,2,1,0:T(8,128)S(1)} %get-tuple-element.126), custom_call_target="InvertDiagBlocksLowerTriangular" | custom-call | tf_op jit(solution)/shard_map/jit(cholesky)/cholesky | solution.py:74
  179.2 11.7 %custom-call.38 = f32[2,64,64]{2,1,0:T(8,128)S(1)} custom-call(f32[2,64,64]{2,1,0:T(8,128)S(1)} %convolution_subtract_fusion.2), custom_call_target="Cholesky" | custom-call | tf_op jit(solution)/shard_map/jit(cholesky)/cholesky | solution.py:74
  191.6 39.5 %custom-call.39 = f32[2,2,128,128]{2,3,1,0:T(8,128)S(1)} custom-call(f32[2,2,128,128]{3,2,1,0:T(8,128)S(1)} %pad_maximum_fusion), custom_call_target="InvertDiagBlocksLowerTriangular" | custom-call | tf_op jit(solution)/shard_map/triangular_solve | solution.py:15
  238.6 4.9 custom-call.40
  245.1 9.7 %copy.124 = f32[2,192,192]{0,2,1:T(8,128)} copy(f32[2,192,192]{2,1,0:T(8,128)S(1)} %get-tuple-element.124) | data formatting | bytes 589824 | tf_op jit(solution)/shard_map/jit(cholesky)/select_n | solution.py:74
  259.7 40.7 %all-gather = f32[32,2,64]{2,1,0:T(2,128)S(1)} all-gather(f32[1,2,64]{2,1,0:T(2,128)S(1)} %fusion.81), channel_id=1, replica_groups=mesh['psr'=8,'toa'=4] {'psr','toa'}, dimensions={0}, use_global_device_ids=true | all-gather | bytes 16896 | tf_op jit(solution)/shard_map/all_gather | solution.py:157
  310.2 376.8 %custom-call.41 = f32[64,64,64]{2,1,0:T(8,128)} custom-call(f32[64,64,64]{2,1,0:T(8,128)} %fusion.26), custom_call_target="Cholesky" | custom-call | tf_op jit(solution)/shard_map/jit(cholesky)/cholesky | solution.py:111
  693.0 67.3 %custom-call.63 = f32[64,1,64,64]{0,2,3,1:T(8,128)S(1)} custom-call(f32[64,1,64,64]{0,3,2,1:T(8,128)} %get-tuple-element.121), custom_call_target="InvertDiagBlocksLowerTriangular" | custom-call | tf_op jit(solution)/shard_map/triangular_solve/custom-call.10 | solution.py:15
  766.3 5.1 convolution_bitcast_fusion.9
  780.2 5.1 convolution_bitcast_fusion.8
  796.5 5.1 convolution_bitcast_fusion.7
  812.5 5.1 convolution_bitcast_fusion.6
  828.5 5.1 convolution_bitcast_fusion.5
  844.4 5.3 convolution_bitcast_fusion.4
  860.6 5.1 convolution_bitcast_fusion.3
  876.5 5.3 convolution_bitcast_fusion.2
  (222 shorter events, 164.6 us)
Async XLA Ops:
  7.2 71.6 %copy-start = (f32[3,64]{1,0:T(4,128)S(1)}, f32[3,64]{1,0:T(4,128)}, u32[]{:S(2)}) copy-start(f32[3,64]{1,0:T(4,128)} %param.21) | copy-start | bytes 2308
  7.2 2.2 copy-start.12
  7.2 2.2 copy-start.13
  7.2 125.7 %all-reduce.6.cloned.1.call-start = ((), (), s32[]{:S(2)}) async-start(), calls=%async_computation | async-start | bytes 4194304 | tf_op jit(solution)/shard_map/psum | solution.py:147
  78.7 13.7 %copy-start.11 = (f32[2,192]{1,0:T(2,128)S(1)}, f32[2,192]{1,0:T(2,128)}, u32[]{:S(2)}) copy-start(f32[2,192]{1,0:T(2,128)} %param.19) | copy-start | bytes 4612
  78.7 221.8 %all-gather.3.cloned.1.call-start = ((), (), s32[]{:S(2)}) async-start(), calls=%async_computation.1 | async-start | bytes 2162688 | tf_op jit(solution)/shard_map/all_gather | solution.py:156
  191.4 52.1 %copy-start.14 = (f32[32]{0:T(128)S(1)}, f32[32]{0:T(128)}, u32[]{:S(2)}) copy-start(f32[32]{0:T(128)} %param.20) | copy-start | bytes 388
  766.2 5.1 copy-start.3
  766.2 8.5 copy-start.2
  780.2 5.1 copy-start.4
  796.5 5.1 copy-start.5
  812.4 5.1 copy-start.6
  828.5 5.1 copy-start.7
  844.4 5.3 copy-start.8
  860.5 5.1 copy-start.9
  876.5 5.4 copy-start.10
  876.5 19.6 %copy-start.1 = (f32[3,64]{1,0:T(4,128)S(1)}, f32[3,64]{1,0:T(4,128)}, u32[]{:S(2)}) copy-start(f32[3,64]{1,0:T(4,128)} %param.21) | copy-start | bytes 2308
Sparse Core Ops, SparseCore 0:
  78.8 54.0 all-reduce.5
  237.4 56.4 all-gather.2
where the time goes:
time: 910 us; the launch traced here: 903 us
  other arithmetic  576 us (63%)
  matrix products  163 us (18%)
  blocking collectives  47.9 us (5%)
  waiting for transfers between devices  40.6 us (4%)
  local copies, waits for them, and re-layouts  39.6 us (4%)
  between operations  35.9 us (4%)
    another operation x3, other arithmetic, block_setup(): block_factor = jnp.linalg.cholesky(block_matrix)  378 us
    another operation x13, other arithmetic, cholesky_solve(): lax.linalg.triangular_solve(factor, halfway, left_side=True, lower=True,...  116 us
    another operation x10, other arithmetic, eliminate(): factor = jnp.linalg.cholesky(own_block)  55.2 us
    another operation x12, matrix products, cholesky_solve(): lax.linalg.triangular_solve(factor, right_side, left_side=True, lower=True)  42.2 us
    all_gather x1, blocking collectives, body(): lax.all_gather(target, ('psr', 'toa'), axis=0, tiled=True)  40.7 us
    psum x1, waiting for transfers between devices, body(): totals = lax.psum((gram_part, fit_part, energy_part, count_part), 'toa')  40.5 us
    dot_general x6, matrix products, slot_term_values(): jnp.einsum('sp,skl->pkl', owners, products, precision=highest)  28.7 us
    another operation x12, matrix products, cholesky_solve(): lax.linalg.triangular_solve(factor, halfway, left_side=True, lower=True,...  28.1 us
  transfers between devices with their start and end apart: 2, of which 1 were waited for; matrix products, arithmetic and copies ran while one was open for 3% of the time, Pallas kernels for 0%

commit v1 on v0

v1 whole, which is shorter than its diff:
```python
import functools

import jax
import jax.numpy as jnp
from jax import lax
from jax.experimental import pallas as pl
from jax.experimental.pallas import tpu as pltpu
from jax.sharding import PartitionSpec as P

GROUP_PULSARS = 8
ITERS = 8
SIDE = 64
STEP_SLOTS = 8
highest = lax.Precision.HIGHEST


def dot(a, b, precision=highest):
    return jnp.dot(a, b, precision=precision, preferred_element_type=jnp.float32)


def gram_kernel(pulsar_ref, rows_ref, design_ref, weight_ref, residual_ref, out_ref):
    step = pl.program_id(0)
    toas, columns = design_ref.shape[1], design_ref.shape[2]

    @pl.when(step == 0)
    def _():
        out_ref[...] = jnp.zeros_like(out_ref)

    lanes = lax.broadcasted_iota(jnp.int32, (1, toas), 1)
    for j in range(STEP_SLOTS):
        slot = step * STEP_SLOTS + j
        p = pulsar_ref[slot]
        valid = lanes < rows_ref[slot]
        weight = jnp.where(valid, weight_ref[j : j + 1, :], 0.0)
        residual = residual_ref[j : j + 1, :].astype(jnp.float32)
        block = design_ref[j]
        across = jnp.transpose(block).astype(jnp.float32)
        weighted = (across * weight).astype(jnp.bfloat16)
        gram = jnp.dot(weighted, block, preferred_element_type=jnp.float32)
        spread = jnp.broadcast_to(residual, (8, toas)).astype(jnp.bfloat16)
        fitted = lax.dot_general(
            spread, weighted, (((1,), (1,)), ((), ())), preferred_element_type=jnp.float32
        )
        energy = weight * residual * residual
        count = jnp.where(valid, 1.0, 0.0)
        tail = jnp.concatenate([energy, count], axis=1)
        at_row = lax.broadcasted_iota(jnp.int32, (8, columns), 0)
        extra = jnp.where(at_row == 0, fitted, jnp.where(at_row == 1, tail, 0.0))
        out_ref[p, 0:columns, :] += gram
        out_ref[p, columns : columns + 8, :] += extra


def local_grams(design, noise_weight, residuals, slot_pulsar, slot_rows):
    slots, toas, columns = design.shape
    return pl.pallas_call(
        gram_kernel,
        grid_spec=pltpu.PrefetchScalarGridSpec(
            num_scalar_prefetch=2,
            grid=(slots // STEP_SLOTS,),
            in_specs=[
                pl.BlockSpec((STEP_SLOTS, toas, columns), lambda i, *_: (i, 0, 0)),
                pl.BlockSpec((STEP_SLOTS, toas), lambda i, *_: (i, 0)),
                pl.BlockSpec((STEP_SLOTS, toas), lambda i, *_: (i, 0)),
            ],
            out_specs=pl.BlockSpec((GROUP_PULSARS, columns + 8, columns), lambda i, *_: (0, 0, 0)),
        ),
        out_shape=jax.ShapeDtypeStruct((GROUP_PULSARS, columns + 8, columns), jnp.float32),
        name="gram",
    )(slot_pulsar, slot_rows, design, noise_weight, residuals)


def invert(mats):
    side = mats[0].shape[0]
    lane = lax.broadcasted_iota(jnp.int32, (1, side), 1)
    sub = lax.broadcasted_iota(jnp.int32, (side, side), 0)
    lane_full = lax.broadcasted_iota(jnp.int32, (side, side), 1)
    pivots = [jnp.ones((1, side), jnp.float32) for _ in mats]
    mats = list(mats)
    for k in range(side):
        for m, a in enumerate(mats):
            row = a[k : k + 1, :]
            col = a[:, k : k + 1]
            pivot = a[k : k + 1, k : k + 1]
            inverse = 1.0 / pivot
            pivots[m] = jnp.where(lane == k, pivot, pivots[m])
            row = jnp.where(lane == k, 1.0, row) * inverse
            kept = jnp.where(lane_full == k, 0.0, a)
            mats[m] = jnp.where(sub == k, row, kept - col * row)
    return mats, [jnp.sum(jnp.log(v), axis=1, keepdims=True) for v in pivots]


def coupling_kernel(directions_ref, out_ref):
    d = directions_ref[...]
    cosines = jnp.clip(
        lax.dot_general(d, d, (((0,), (0,)), ((), ())), precision=highest, preferred_element_type=jnp.float32),
        -1.0,
        1.0,
    )
    number = cosines.shape[0]
    row = lax.broadcasted_iota(jnp.int32, (number, number), 0)
    col = lax.broadcasted_iota(jnp.int32, (number, number), 1)
    spread = jnp.where(row == col, 1.0, 0.5 * (1.0 - cosines))
    curve = 1.5 * spread * jnp.log(spread) - 0.25 * spread + 0.5
    x = jnp.where(row == col, 1.0, curve)
    side = min(SIDE, number)
    for b in range(number // side):
        lo, hi = b * side, (b + 1) * side
        (inverse,), _ = invert([x[lo:hi, lo:hi]])
        if number == side:
            x = inverse
            continue
        across = dot(inverse, x[lo:hi, :])
        down = x[:, lo:hi]
        inside_row = (row >= lo) & (row < hi)
        inside_col = (col >= lo) & (col < hi)
        updated = x - dot(down, across)
        placed = -dot(down, inverse)
        tiles = number // side
        updated = jnp.where(inside_col, jnp.concatenate([placed] * tiles, axis=1), updated)
        fixed = jnp.where(inside_col, jnp.concatenate([jnp.concatenate([inverse] * tiles, axis=1)] * tiles, axis=0),
                          jnp.concatenate([across] * tiles, axis=0))
        x = jnp.where(inside_row, fixed, updated)
    out_ref[...] = x


def coupling_inverse(directions):
    number = directions.shape[1]
    padded = jnp.pad(directions, ((0, 8 - directions.shape[0]), (0, 0)))
    return pl.pallas_call(
        coupling_kernel,
        out_shape=jax.ShapeDtypeStruct((number, number), jnp.float32),
        cost_estimate=pl.CostEstimate(flops=number**3 * 60, bytes_accessed=4 * number * number, transcendentals=0),
        name="coupling",
    )(padded)


def eliminate_kernel(toa_devices, sums_ref, prior_ref, coupling_ref, power_ref, packed_ref, extra_ref, work_ref):
    owned, height, columns = sums_ref.shape
    common = columns - prior_ref.shape[2]
    device = lax.axis_index("psr") * toa_devices + lax.axis_index("toa")
    row = lax.broadcasted_iota(jnp.int32, (height, columns), 0)
    col = lax.broadcasted_iota(jnp.int32, (height, columns), 1)
    energies, counts = [], []
    for i in range(owned):
        diag = jnp.concatenate([jnp.zeros((1, common), jnp.float32), 1.0 / prior_ref[i]], axis=1)
        tail = sums_ref[i, columns + 1 : columns + 2, :]
        energies.append(jnp.sum(tail[:, : columns // 2], axis=1, keepdims=True))
        counts.append(jnp.sum(tail[:, columns // 2 :], axis=1, keepdims=True))
        work_ref[i] = sums_ref[i] + jnp.where(row == col, diag, 0.0)
    logs = [jnp.zeros((1, 1), jnp.float32)] * owned
    quads = [jnp.zeros((1, 1), jnp.float32)] * owned
    for lo in range(common, columns, SIDE):
        hi = lo + SIDE
        inverses, extra_logs = invert([work_ref[i, lo:hi, lo:hi] for i in range(owned)])
        for i in range(owned):
            logs[i] = logs[i] + extra_logs[i]
            down = work_ref[i, :, lo:hi]
            scaled = dot(down, inverses[i])
            quads[i] = quads[i] + jnp.sum(
                scaled[columns : columns + 1] * down[columns : columns + 1], axis=1, keepdims=True
            )
            work_ref[i] = work_ref[i] - dot(scaled, work_ref[i, lo:hi, :])
    lane_p = lax.broadcasted_iota(jnp.int32, (1, coupling_ref.shape[1]), 1)
    rc = lax.broadcasted_iota(jnp.int32, (common, common), 0)
    cc = lax.broadcasted_iota(jnp.int32, (common, common), 1)
    blocks = []
    for i in range(owned):
        p = device * owned + i
        own = jnp.sum(jnp.where(lane_p == p, coupling_ref[pl.ds(p, 1), :], 0.0), axis=1, keepdims=True)
        blocks.append(work_ref[i, :common, :common] + jnp.where(rc == cc, own * power_ref[...], 0.0))
    inverses, block_logs = invert(blocks)
    half = common // 2
    lane = lax.broadcasted_iota(jnp.int32, (1, 128 - common), 1)
    for i in range(owned):
        packed_ref[i, 0:half, :] = jnp.concatenate([inverses[i][:half], inverses[i][half:]], axis=1)
        target = work_ref[i, columns : columns + 1, :common]
        facts = jnp.where(lane == 0, (logs[i] + block_logs[i]) / columns, 0.0)
        facts = jnp.where(lane == 1, energies[i] - quads[i], facts)
        facts = jnp.where(lane == 2, counts[i], facts)
        line = jnp.concatenate([target, facts], axis=1)
        packed_ref[i, half : half + 8, :] = jnp.broadcast_to(line, (8, 128))
        extra_ref[i : i + 1, :] = line


def eliminate(sums, own_prior, coupling, power, toa_devices):
    owned, height, columns = sums.shape
    common = columns - own_prior.shape[1]
    return pl.pallas_call(
        functools.partial(eliminate_kernel, toa_devices),
        out_shape=(
            jax.ShapeDtypeStruct((owned, common // 2 + 8, 2 * common), jnp.float32),
            jax.ShapeDtypeStruct((owned, 2 * common), jnp.float32),
        ),
        scratch_shapes=[pltpu.VMEM((owned, height, columns), jnp.float32)],
        name="eliminate",
    )(sums, own_prior[:, None, :], coupling, power)


def conjugate_kernel(packed_ref, coupling_ref, power_ref, out_ref, blocks_ref, w_ref):
    number = coupling_ref.shape[0]
    common = power_ref.shape[0]
    half = common // 2
    stride = half + 8

    def spread(k, carry):
        x = jnp.transpose(packed_ref[pl.ds(k, number, stride=stride), :])
        blocks_ref[k] = x[:common]
        blocks_ref[k + half] = x[common:]
        return carry

    lax.fori_loop(0, half, spread, 0)
    target = jnp.transpose(packed_ref[pl.ds(half, number, stride=stride), :])[:common]
    row = lax.broadcasted_iota(jnp.int32, (number, number), 0)
    col = lax.broadcasted_iota(jnp.int32, (number, number), 1)
    mixing = jnp.where(row == col, 0.0, coupling_ref[...])
    power = power_ref[...]

    def total(x):
        return jnp.sum(jnp.sum(x, axis=0, keepdims=True), axis=1, keepdims=True)

    def apply_blocks(v):
        w_ref[...] = v
        acc = jnp.zeros((common, number), jnp.float32)
        for k in range(common):
            acc = acc + blocks_ref[k] * w_ref[k : k + 1, :]
        return acc

    solution = jnp.zeros((common, number), jnp.float32)
    residual = target
    scaled = apply_blocks(residual)
    direction, block_direction = scaled, residual
    inner = total(residual * scaled)
    for iteration in range(ITERS):
        coupled = power * dot(direction, mixing)
        mapped = block_direction + coupled
        step = inner / total(direction * mapped)
        solution = solution + step * direction
        if iteration + 1 < ITERS:
            residual = residual - step * mapped
            scaled = scaled - step * (direction + apply_blocks(coupled))
            following = total(residual * scaled)
            ratio = following / inner
            direction = scaled + ratio * direction
            block_direction = residual + ratio * block_direction
            inner = following
    out_ref[...] = jnp.transpose(solution)


def conjugate(packed, coupling, power):
    number = coupling.shape[0]
    common = power.shape[0]
    return pl.pallas_call(
        conjugate_kernel,
        out_shape=jax.ShapeDtypeStruct((number, common), jnp.float32),
        scratch_shapes=[
            pltpu.VMEM((common, common, number), jnp.float32),
            pltpu.VMEM((common, number), jnp.float32),
        ],
        name="conjugate",
    )(packed.reshape(-1, packed.shape[-1]), coupling, power)


def body(design, noise_weight, residuals, slot_pulsar, slot_rows, own_prior, spectrum, directions):
    toa_devices = lax.axis_size("toa")
    owned = GROUP_PULSARS // toa_devices
    device = lax.axis_index("psr") * toa_devices + lax.axis_index("toa")
    partial = local_grams(design, noise_weight, residuals, slot_pulsar, slot_rows)
    sums = lax.psum_scatter(partial, "toa", scatter_dimension=0, tiled=True)
    coupling = coupling_inverse(directions)
    power = 1.0 / jnp.repeat(spectrum, 2)
    packed, extra = eliminate(sums, own_prior, coupling, power[None, :], toa_devices)
    everything = lax.all_gather(packed, ("psr", "toa"), axis=0, tiled=True)
    whole = conjugate(everything, coupling, power[:, None])
    common = whole.shape[1]
    solution = lax.dynamic_slice_in_dim(whole, device * owned, owned, 0)
    chi_square = (extra[:, common + 1] - jnp.sum(extra[:, :common] * solution, axis=1)) / extra[:, common + 2]
    return (solution, extra[:, common], chi_square)


def solution(mesh):
    return jax.shard_map(
        body,
        mesh=mesh,
        in_specs=(
            P(("psr", "toa"), None, None),
            P(("psr", "toa"), None),
            P(("psr", "toa"), None),
            P(("psr", "toa")),
            P(("psr", "toa")),
            P(("psr", "toa"), None),
            P(),
            P(),
        ),
        out_specs=(P(("psr", "toa"), None), P(("psr", "toa")), P(("psr", "toa"))),
        check_vma=False,
    )
```

time: 910 us -> 155 us (0.17)
  other arithmetic: 576 us -> 1.88 us
  matrix products: 163 us -> 0 us
  Pallas kernels: 0 us -> 56.2 us
  blocking collectives: 47.9 us -> 0 us
  waiting for transfers between devices: 40.6 us -> 77.4 us
  local copies, waits for them, and re-layouts: 39.6 us -> 4.64 us
  between operations: 35.9 us -> 14.1 us
    another operation x29 -> x0, other arithmetic: 555 us -> none  [the longest x3 378 us: block_setup(): block_factor = jnp.linalg.cholesky(block_matrix)]
    dot_general x54 -> x0, matrix products: 91.9 us -> none  [the longest x6 28.7 us: slot_term_values(): jnp.einsum('sp,skl->pkl', owners, products, precision=highest)]
    another operation x26 -> x0, matrix products: 70.8 us -> none  [the longest x12 42.2 us: cholesky_solve(): lax.linalg.triangular_solve(factor, right_side, left_side=True, lower=True)]
    pallas_call x0 -> x4, Pallas kernels: none -> 56.2 us  [the longest x1 27.8 us: eliminate(): pl.pallas_call(functools.partial(eliminate_kernel, toa_devices), out_shap...]
    all_gather x1, waiting for transfers between devices: 0.01 us -> 52.3 us  [body(): everything = lax.all_gather(packed, ('psr', 'toa'), axis=0, tiled=True)]
    all_gather x1 -> x0, blocking collectives: 40.7 us -> none  [body(): lax.all_gather(target, ('psr', 'toa'), axis=0, tiled=True)]
    psum x1 -> x0, waiting for transfers between devices: 40.5 us -> none  [body(): totals = lax.psum((gram_part, fit_part, energy_part, count_part), 'toa')]
    reduce_scatter x0 -> x1, waiting for transfers between devices: none -> 25 us  [body(): sums = lax.psum_scatter(partial, 'toa', scatter_dimension=0, tiled=True)]
  transfers between devices with their start and end apart: 2 -> 2, of which waited for: 1 -> 2; matrix products, arithmetic and copies ran while one was open for 3% -> 3% of each run, Pallas kernels for 0% -> 4%
where the time goes in v1:
time: 155 us; the launch traced here: 154 us
  waiting for transfers between devices  77.4 us (50%)
  Pallas kernels  56.2 us (36%)
  between operations  14.1 us (9%)
  local copies, waits for them, and re-layouts  4.64 us (3%)
  other arithmetic  1.88 us (1%)
    all_gather x1, waiting for transfers between devices, body(): everything = lax.all_gather(packed, ('psr', 'toa'), axis=0, tiled=True)  52.3 us
    pallas_call x1, Pallas kernels, eliminate(): pl.pallas_call(functools.partial(eliminate_kernel, toa_devices), out_shap...  27.8 us
    reduce_scatter x1, waiting for transfers between devices, body(): sums = lax.psum_scatter(partial, 'toa', scatter_dimension=0, tiled=True)  25 us
    pallas_call x1, Pallas kernels, local_grams(): pl.pallas_call(gram_kernel, grid_spec=pltpu.PrefetchScalarGridSpec(num_sc...  12.9 us
    pallas_call x1, Pallas kernels, conjugate(): pl.pallas_call(conjugate_kernel, out_shape=jax.ShapeDtypeStruct((number,...  8.65 us
    pallas_call x1, Pallas kernels, coupling_inverse(): pl.pallas_call(coupling_kernel, out_shape=jax.ShapeDtypeStruct((number, n...  6.94 us
  transfers between devices with their start and end apart: 2, of which 2 were waited for; matrix products, arithmetic and copies ran while one was open for 3% of the time, Pallas kernels for 4%

profile of v1, /device:TPU:0, one launch (start us, length us, event | category | flops | bytes accessed | tf_op | source)
XLA Modules:
  0.0 154.3 jit_solution(10210291945807729840)
XLA Ops:
  7.2 0.0 reduce-scatter.2.cloned.1.call-start
  7.2 12.9 %gram.1 = f32[8,264,256]{2,1,0:T(8,128)} custom-call(s32[96]{0:T(128)} %pulsar_ref.1, s32[96]{0:T(128)} %rows_ref.1, bf16[96,128,256]{2,1,0:T(8,128)(2,1)} %design_ref.1, f32[96,128]{1,0:T(8,128)} %weight_ref.1, bf16[96,128]{1,0:T(8,128)(2,1)} %residual_ref.1), custom_call_target="tpu_custom_call" | custom-call | tf_op jit(solution)/shard_map/gram/pallas_call | solution.py:55
  20.1 0.0 copy-start
  20.1 0.0 copy-start.2
  20.1 0.0 copy-start.1
  20.1 0.0 reduce-scatter.2.cloned.1.call-update
  20.1 0.0 all-gather.2.cloned.1.call-start
  20.2 0.6 copy-done
  20.8 0.6 broadcast_in_dim.8.prior_ref
  21.4 0.0 copy-done.2
  21.4 0.1 broadcast_in_dim.9
  21.4 0.6 div.33.power_ref
  22.1 0.0 copy-done.1
  22.1 0.6 pad.4.directions_ref
  22.7 6.9 %coupling.1.coupling_ref = f32[64,64]{1,0:T(8,128)} custom-call(f32[8,64]{1,0:T(8,128)} %pad.4.directions_ref), custom_call_target="tpu_custom_call" | custom-call | flops 15728640 | bytes 16384 | tf_op jit(solution)/shard_map/coupling/pallas_call | solution.py:129
  29.6 25.0 %reduce-scatter.2.cloned.1.call-done.sums_ref = f32[2,264,256]{2,1,0:T(8,128)} async-done(((f32[8,264,256]{2,1,0:T(8,128)}), f32[2,264,256]{2,1,0:T(8,128)}) %reduce-scatter.2.cloned.1.call-update) | async-done | bytes 540688 | tf_op jit(solution)/shard_map/reduce_scatter | solution.py:268
  54.7 27.8 %eliminate.1 = (f32[2,40,128]{2,1,0:T(8,128)}, f32[2,128]{1,0:T(2,128)}) custom-call(f32[2,264,256]{2,1,0:T(8,128)} %reduce-scatter.2.cloned.1.call-done.sums_ref, f32[2,1,192]{2,1,0:T(1,128)} %broadcast_in_dim.8.prior_ref, f32[64,64]{1,0:T(8,128)} %coupling.1.coupling_ref, f32[1,64]{1,0:T(1,128)} %div.33.power_ref), custom_call_target="tpu_custom_call" | custom-call | tf_op jit(solution)/shard_map/eliminate/pallas_call | solution.py:188
  82.4 0.0 all-gather.2.cloned.1.call-update
  82.4 0.7 div.36.power_ref
  83.1 1.5 slice_reduce_fusion.1
  84.6 52.3 %all-gather.2.cloned.1.call-done = f32[64,40,128]{2,1,0:T(8,128)} async-done(((f32[2,40,128]{2,1,0:T(8,128)}), f32[64,40,128]{2,1,0:T(8,128)}) %all-gather.2.cloned.1.call-update) | async-done | bytes 1310736 | tf_op jit(solution)/shard_map/all_gather | solution.py:272
  136.9 8.7 %conjugate.1 = f32[64,64]{1,0:T(8,128)} custom-call(f32[2560,128]{1,0:T(8,128)} %bitcast.1, f32[64,64]{1,0:T(8,128)} %coupling.1.coupling_ref, f32[64,1]{1,0:T(8,128)} %div.36.power_ref), custom_call_target="tpu_custom_call" | custom-call | tf_op jit(solution)/shard_map/conjugate/pallas_call | solution.py:252
  145.6 1.4 multiply_reduce_fusion
  146.9 0.5 subtract_divide_fusion
  (1 shorter events, 0.0 us)
Async XLA Ops:
  7.2 47.5 %reduce-scatter.2.cloned.1.call-start = ((), (), s32[]{:S(2)}) async-start(), calls=%async_computation.1 | async-start | bytes 2703360 | tf_op jit(solution)/shard_map/reduce_scatter | solution.py:268
  20.1 0.7 copy-start
  20.1 1.3 copy-start.2
  20.1 2.0 %copy-start.1 = (f32[3,64]{1,0:T(4,128)S(1)}, f32[3,64]{1,0:T(4,128)}, u32[]{:S(2)}) copy-start(f32[3,64]{1,0:T(4,128)} %param.15) | copy-start | bytes 2308
  20.1 116.8 %all-gather.2.cloned.1.call-start = ((), (), s32[]{:S(2)}) async-start(), calls=%async_computation.2 | async-start | bytes 1351680 | tf_op jit(solution)/shard_map/all_gather | solution.py:272
Sparse Core Ops, SparseCore 0:
  20.3 34.3 reduce-scatter.1
  82.6 54.3 all-gather.1

commit v2 on v1

--- a/solution.py
+++ b/solution.py
@@ -260,16 +260,184 @@
     )(packed.reshape(-1, packed.shape[-1]), coupling, power)
 
 
+MESH = pl.DeviceIdType.MESH
+
+
+def reduce_kernel(chips, partial_ref, out_ref, near_ref, sum_ref, far_ref, near_send, near_recv, far_send, far_recv):
+    me = lax.axis_index("toa")
+    core = lax.rem(me, 2)
+    chip = me // 2
+    other = 1 - core
+    owned = out_ref.shape[0]
+    barrier = pltpu.get_barrier_semaphore()
+    pl.semaphore_signal(barrier, inc=1, device_id={"toa": chip * 2 + other}, device_id_type=MESH)
+    for d in range(1, chips):
+        target = lax.rem(chip + d, chips) * 2 + core
+        pl.semaphore_signal(barrier, inc=1, device_id={"toa": target}, device_id_type=MESH)
+    pl.semaphore_wait(barrier, chips)
+    order = [d % chips for d in range(1, chips + 1)]
+    near, far = {}, {}
+    for d in order:
+        owner = lax.rem(chip + d, chips) * 2 + other
+        for i in range(owned):
+            near[d, i] = pltpu.make_async_remote_copy(
+                src_ref=partial_ref.at[owner * owned + i],
+                dst_ref=near_ref.at[d * owned + i],
+                send_sem=near_send.at[d * owned + i],
+                recv_sem=near_recv.at[d * owned + i],
+                device_id={"toa": chip * 2 + other},
+                device_id_type=MESH,
+            )
+            near[d, i].start()
+    for d in order:
+        owner = lax.rem(chip + d, chips) * 2 + core
+        for i in range(owned):
+            at = d * owned + i
+            near[d, i].wait_recv()
+            both = partial_ref[owner * owned + i] + near_ref[at]
+            if d == 0:
+                out_ref[i] = both
+                continue
+            sum_ref[at - owned] = both
+            far[d, i] = pltpu.make_async_remote_copy(
+                src_ref=sum_ref.at[at - owned],
+                dst_ref=far_ref.at[at - owned],
+                send_sem=far_send.at[at - owned],
+                recv_sem=far_recv.at[at - owned],
+                device_id={"toa": owner},
+                device_id_type=MESH,
+            )
+            far[d, i].start()
+    for (d, i), copy in far.items():
+        copy.wait_recv()
+        out_ref[i] += far_ref[d * owned + i - owned]
+    for copy in list(near.values()) + list(far.values()):
+        copy.wait_send()
+
+
+def reduce_owners(partial, toa_devices):
+    pulsars, height, columns = partial.shape
+    owned = pulsars // toa_devices
+    chips = toa_devices // 2
+    moved = owned * (chips - 1)
+    block = (height, columns)
+    return pl.pallas_call(
+        functools.partial(reduce_kernel, chips),
+        out_shape=jax.ShapeDtypeStruct((owned,) + block, jnp.float32),
+        in_specs=[pl.BlockSpec(memory_space=pltpu.VMEM)],
+        out_specs=pl.BlockSpec(memory_space=pltpu.VMEM),
+        scratch_shapes=[
+            pltpu.VMEM((owned * chips,) + block, jnp.float32),
+            pltpu.VMEM((moved,) + block, jnp.float32),
+            pltpu.VMEM((moved,) + block, jnp.float32),
+            pltpu.SemaphoreType.DMA((owned * chips,)),
+            pltpu.SemaphoreType.DMA((owned * chips,)),
+            pltpu.SemaphoreType.DMA((moved,)),
+            pltpu.SemaphoreType.DMA((moved,)),
+        ],
+        compiler_params=pltpu.CompilerParams(collective_id=0, has_side_effects=True),
+        cost_estimate=pl.CostEstimate(flops=4 * pulsars * height * columns, bytes_accessed=40 * pulsars * height * columns, transcendentals=0),
+        name="reduce_owners",
+    )(partial)
+
+
+def gather_kernel(groups, chips, mine_ref, out_ref, all_ref, psr_send, chip_send, core_send, recv):
+    psr, me = lax.axis_index("psr"), lax.axis_index("toa")
+    toa_devices = 2 * chips
+    core = lax.rem(me, 2)
+    chip = me // 2
+    other = 1 - core
+    partner = chip * 2 + other
+    barrier = pltpu.get_barrier_semaphore()
+
+    def greet(psr_to, toa_to):
+        pl.semaphore_signal(barrier, inc=1, device_id={"psr": psr_to, "toa": toa_to}, device_id_type=MESH)
+
+    greet(psr, partner)
+    for d in range(1, chips):
+        greet(psr, lax.rem(chip + d, chips) * 2 + core)
+    for e in range(1, groups):
+        greet(lax.rem(psr + e, groups), me)
+    pl.semaphore_wait(barrier, chips + groups - 1)
+    sent = []
+
+    def block_of(e, toa):
+        return lax.rem(psr + groups - e, groups) * toa_devices + toa
+
+    def copy(source, block, sem, psr_to, toa_to):
+        return pltpu.make_async_remote_copy(
+            src_ref=source,
+            dst_ref=all_ref.at[block],
+            send_sem=sem,
+            recv_sem=recv.at[block],
+            device_id={"psr": psr_to, "toa": toa_to},
+            device_id_type=MESH,
+        )
+
+    def send(source, block, sem, psr_to, toa_to):
+        moving = copy(source, block, sem, psr_to, toa_to)
+        moving.start()
+        sent.append(moving)
+
+    def arrived(block):
+        copy(all_ref.at[block], block, core_send.at[0], psr, partner).wait_recv()
+
+    own = psr * toa_devices + me
+    for e in range(1, groups):
+        send(mine_ref, own, psr_send.at[e - 1], lax.rem(psr + e, groups), me)
+    for e in range(groups):
+        block = block_of(e, me)
+        if e:
+            arrived(block)
+        source = all_ref.at[block] if e else mine_ref
+        for d in range(1, chips):
+            send(source, block, chip_send.at[e * (chips - 1) + d - 1], psr, lax.rem(chip + d, chips) * 2 + core)
+        send(source, block, core_send.at[e], psr, partner)
+    for d in range(1, chips):
+        for e in range(groups):
+            block = block_of(e, lax.rem(chip + chips - d, chips) * 2 + core)
+            arrived(block)
+            send(all_ref.at[block], block, core_send.at[d * groups + e], psr, partner)
+    all_ref[own] = mine_ref[...]
+    for c in range(chips):
+        for e in range(groups):
+            arrived(block_of(e, c * 2 + other))
+    for moving in sent:
+        moving.wait_send()
+    out_ref[...] = all_ref[...]
+
+
+def gather_all(mine, groups, toa_devices):
+    chips = toa_devices // 2
+    devices = groups * toa_devices
+    return pl.pallas_call(
+        functools.partial(gather_kernel, groups, chips),
+        out_shape=jax.ShapeDtypeStruct((devices,) + mine.shape, jnp.float32),
+        in_specs=[pl.BlockSpec(memory_space=pltpu.VMEM)],
+        out_specs=pl.BlockSpec(memory_space=pltpu.VMEM),
+        scratch_shapes=[
+            pltpu.VMEM((devices,) + mine.shape, jnp.float32),
+            pltpu.SemaphoreType.DMA((groups - 1,)),
+            pltpu.SemaphoreType.DMA((groups * (chips - 1),)),
+            pltpu.SemaphoreType.DMA((groups * chips,)),
+            pltpu.SemaphoreType.DMA((devices,)),
+        ],
+        compiler_params=pltpu.CompilerParams(collective_id=1, has_side_effects=True),
+        name="gather_all",
+    )(mine)
+
+
 def body(design, noise_weight, residuals, slot_pulsar, slot_rows, own_prior, spectrum, directions):
     toa_devices = lax.axis_size("toa")
     owned = GROUP_PULSARS // toa_devices
     device = lax.axis_index("psr") * toa_devices + lax.axis_index("toa")
     partial = local_grams(design, noise_weight, residuals, slot_pulsar, slot_rows)
-    sums = lax.psum_scatter(partial, "toa", scatter_dimension=0, tiled=True)
+    sums = reduce_owners(partial, toa_devices)
     coupling = coupling_inverse(directions)
     power = 1.0 / jnp.repeat(spectrum, 2)
     packed, extra = eliminate(sums, own_prior, coupling, power[None, :], toa_devices)
-    everything = lax.all_gather(packed, ("psr", "toa"), axis=0, tiled=True)
+    mine = packed.reshape(-1, packed.shape[-1])
+    everything = gather_all(mine, lax.axis_size("psr"), toa_devices)
     whole = conjugate(everything, coupling, power[:, None])
     common = whole.shape[1]
     solution = lax.dynamic_slice_in_dim(whole, device * owned, owned, 0)

time: 155 us -> 102 us (0.66)
  waiting for transfers between devices: 77.4 us -> 0 us
  Pallas kernels: 56.2 us -> 95.6 us
  between operations: 14.1 us -> 0.67 us
    all_gather x1 -> x0, waiting for transfers between devices: 52.3 us -> none  [body(): everything = lax.all_gather(packed, ('psr', 'toa'), axis=0, tiled=True)]
    pallas_call x0 -> x2, Pallas kernels: none -> 39.4 us  [the longest x1 19.8 us: gather_all(): pl.pallas_call(functools.partial(gather_kernel, groups, chips), out_shape...]
    reduce_scatter x1 -> x0, waiting for transfers between devices: 25 us -> none  [body(): sums = lax.psum_scatter(partial, 'toa', scatter_dimension=0, tiled=True)]
  transfers between devices with their start and end apart: 2 -> 0, of which waited for: 2 -> 0; matrix products, arithmetic and copies ran while one was open for 3% -> 0% of each run, Pallas kernels for 4% -> 0%
where the time goes in v2:
time: 102 us; the launch traced here: 101 us
  Pallas kernels  95.6 us (94%)
  local copies, waits for them, and re-layouts  3.27 us (3%)
  other arithmetic  1.88 us (2%)
    pallas_call x1, Pallas kernels, eliminate(): pl.pallas_call(functools.partial(eliminate_kernel, toa_devices), out_shap...  27.8 us
    pallas_call x1, Pallas kernels, gather_all(): pl.pallas_call(functools.partial(gather_kernel, groups, chips), out_shape...  19.8 us
    pallas_call x1, Pallas kernels, reduce_owners(): pl.pallas_call(functools.partial(reduce_kernel, chips), out_shape=jax.Sha...  19.6 us
    pallas_call x1, Pallas kernels, local_grams(): pl.pallas_call(gram_kernel, grid_spec=pltpu.PrefetchScalarGridSpec(num_sc...  12.9 us
    pallas_call x1, Pallas kernels, conjugate(): pl.pallas_call(conjugate_kernel, out_shape=jax.ShapeDtypeStruct((number,...  8.67 us
    pallas_call x1, Pallas kernels, coupling_inverse(): pl.pallas_call(coupling_kernel, out_shape=jax.ShapeDtypeStruct((number, n...  6.95 us

profile of v2, /device:TPU:0, one launch (start us, length us, event | category | flops | bytes accessed | tf_op | source)
XLA Modules:
  0.0 101.5 jit_solution(1325230494462956786)
XLA Ops:
  0.6 12.9 %gram.1.partial_ref = f32[8,264,256]{2,1,0:T(8,128)} custom-call(s32[96]{0:T(128)} %pulsar_ref.1, s32[96]{0:T(128)} %rows_ref.1, bf16[96,128,256]{2,1,0:T(8,128)(2,1)} %design_ref.1, f32[96,128]{1,0:T(8,128)} %weight_ref.1, bf16[96,128]{1,0:T(8,128)(2,1)} %residual_ref.1), custom_call_target="tpu_custom_call" | custom-call | tf_op jit(solution)/shard_map/gram/pallas_call | solution.py:55
  13.5 0.0 copy-start.1
  13.5 0.0 copy-start.2
  13.5 0.0 copy-start.3
  13.5 19.6 %reduce_owners.1.sums_ref = f32[2,264,256]{2,1,0:T(8,128)} custom-call(f32[8,264,256]{2,1,0:T(8,128)} %gram.1.partial_ref), custom_call_target="tpu_custom_call" | custom-call | flops 2162688 | bytes 21626880 | tf_op jit(solution)/shard_map/reduce_owners/pallas_call | solution.py:324
  33.1 0.0 copy-done.1
  33.1 0.6 broadcast_in_dim.8.prior_ref
  33.7 0.0 copy-done.2
  33.7 0.6 pad.4.directions_ref
  34.3 6.9 %coupling.1.coupling_ref = f32[64,64]{1,0:T(8,128)} custom-call(f32[8,64]{1,0:T(8,128)} %pad.4.directions_ref), custom_call_target="tpu_custom_call" | custom-call | flops 15728640 | bytes 16384 | tf_op jit(solution)/shard_map/coupling/pallas_call | solution.py:129
  41.3 0.0 copy-done.3
  41.3 0.1 broadcast_in_dim.9
  41.4 0.6 div.33.power_ref
  42.0 27.8 %eliminate.1 = (f32[2,40,128]{2,1,0:T(8,128)}, f32[2,128]{1,0:T(2,128)}) custom-call(f32[2,264,256]{2,1,0:T(8,128)} %reduce_owners.1.sums_ref, f32[2,1,192]{2,1,0:T(1,128)} %broadcast_in_dim.8.prior_ref, f32[64,64]{1,0:T(8,128)} %coupling.1.coupling_ref, f32[1,64]{1,0:T(1,128)} %div.33.power_ref), custom_call_target="tpu_custom_call" | custom-call | tf_op jit(solution)/shard_map/eliminate/pallas_call | solution.py:188
  69.8 0.0 copy-start
  69.8 19.8 %gather_all.1 = f32[32,80,128]{2,1,0:T(8,128)} custom-call(f32[80,128]{1,0:T(8,128)} %bitcast.3), custom_call_target="tpu_custom_call" | custom-call | tf_op jit(solution)/shard_map/gather_all/pallas_call | solution.py:413
  89.5 0.7 div.36.power_ref
  90.2 8.7 %conjugate.1 = f32[64,64]{1,0:T(8,128)} custom-call(f32[2560,128]{1,0:T(8,128)} %bitcast.2, f32[64,64]{1,0:T(8,128)} %coupling.1.coupling_ref, f32[64,1]{1,0:T(8,128)} %div.36.power_ref), custom_call_target="tpu_custom_call" | custom-call | tf_op jit(solution)/shard_map/conjugate/pallas_call | solution.py:252
  98.9 0.0 copy-done
  98.9 1.4 %multiply_reduce_fusion = (f32[2]{0:T(128)S(1)}, f32[2,64]{1,0:T(2,128)}) fusion(f32[2,128]{1,0:T(2,128)S(1)} %copy-done, f32[64,64]{1,0:T(8,128)} %conjugate.1, s32[]{:T(128)S(6)} %select_n.3), kind=kLoop, calls=%fused_computation.1 | loop fusion | flops 254 | bytes 1548 | tf_op jit(solution)/shard_map/reduce_sum | solution.py:444
  100.2 0.7 slice_reduce_fusion.1
  100.9 0.5 subtract_divide_fusion
  (1 shorter events, 0.0 us)
Async XLA Ops:
  13.5 19.6 %copy-start.1 = (f32[2,192]{1,0:T(2,128)S(1)}, f32[2,192]{1,0:T(2,128)}, u32[]{:S(2)}) copy-start(f32[2,192]{1,0:T(2,128)} %param.13) | copy-start | bytes 4612
  13.5 20.2 %copy-start.2 = (f32[3,64]{1,0:T(4,128)S(1)}, f32[3,64]{1,0:T(4,128)}, u32[]{:S(2)}) copy-start(f32[3,64]{1,0:T(4,128)} %param.15) | copy-start | bytes 2308
  13.5 27.8 %copy-start.3 = (f32[32]{0:T(128)S(1)}, f32[32]{0:T(128)}, u32[]{:S(2)}) copy-start(f32[32]{0:T(128)} %param.14) | copy-start | bytes 388
  69.8 29.1 %copy-start = (f32[2,128]{1,0:T(2,128)S(1)}, f32[2,128]{1,0:T(2,128)}, u32[]{:S(2)}) copy-start(f32[2,128]{1,0:T(2,128)} %get-tuple-element.6) | copy-start | bytes 3076
